TPU v7x, 128 devices: a whole 4x4x4 slice. The times are simulated.
128 devices in a mesh: samp: 4 (over z), row: 4 (over x_lo, core), col: 8 (over x_hi, y).
Axes of the slice: x: 4 (x_hi: 2, x_lo: 2; x = x_hi * 2 + x_lo), y: 4, z: 4, core: 2. Of those that a mesh axis runs over, the one named last changes fastest.
Arguments:
- pair: float32 [4, 320, 320, 128], P('samp', 'row', 'col'), may hold values from -6 to 6
- cotangent: float32 [4, 320, 320, 128], P('samp', 'row', 'col'), may hold values from -6 to 6
- crop_length: int32 [4], P('samp'), may hold values from 160 to 320
- in_gain: float32 [128], replicated, may hold values from 0.5 to 1.5
- in_bias: float32 [128], replicated, may hold values from -1.5 to 1.5
- proj_weight: bfloat16 [128, 512], replicated, may hold values from -0.5 to 0.5
- gate_weight: bfloat16 [128, 128], replicated, may hold values from -0.5 to 0.5
- out_gain: float32 [128], replicated, may hold values from 0.5 to 1.5
- out_bias: float32 [128], replicated, may hold values from -1.5 to 1.5
- out_weight: bfloat16 [128, 128], replicated, may hold values from -0.5 to 0.5
Outputs:
- grad_pair: float32 [4, 320, 320, 128], P('samp', 'row', 'col')
- grad_in_gain: float32 [128], replicated
- grad_in_bias: float32 [128], replicated
- grad_proj_weight: float32 [128, 512], replicated
- grad_gate_weight: float32 [128, 128], replicated
- grad_out_gain: float32 [128], replicated
- grad_out_bias: float32 [128], replicated
- grad_out_weight: float32 [128, 128], replicated
All inputs are finite; a program needn't handle non-finite values.
Results may differ from a plain program's by a relative error of at most 0.012.
Values may be sent and summed in bfloat16 or wider, within the bound.
No kernel may reach another device: no remote copies, remote signals or barrier semaphores. Data moves between devices by JAX's collectives and lax.ppermute only.
A program may use at most 128 MiB of HBM per device.

v0:
```python
import jax
import jax.numpy as jnp
from jax import lax
from jax.sharding import PartitionSpec as P

epsilon = 1e-05


def cut_along(shard, dim, length):
    before, after = (shard.shape[:dim], shard.shape[dim + 1 :])
    return jnp.moveaxis(shard.reshape(*before, length, -1, *after), dim, 0)


def piece_ends(length, count):
    unit = 8 if length >= 8 * count else 1
    return [length // unit * k // count * unit for k in range(1, count)]


def joined_along(parts, dim):
    parts = jnp.moveaxis(parts, 0, dim)
    lengths = parts.shape
    return parts.reshape(*lengths[:dim], lengths[dim] * lengths[dim + 1], *lengths[dim + 2 :])


def cut_exchange(shard, axis, pieces, split_dim, concat_dim):
    parts = cut_along(shard, split_dim, lax.axis_size(axis))
    widest = max(range(1, max(2, parts.ndim - 1)), key=lambda d: parts.shape[d])
    finished = []
    for share in jnp.split(parts, piece_ends(parts.shape[widest], pieces), axis=widest):
        if share.size:
            finished.append(lax.all_to_all(share, axis, split_axis=0, concat_axis=0, tiled=True))
    return joined_along(jnp.concatenate(finished, axis=widest), concat_dim)


def packed_total(arrays, axis):
    line, at, finished = (jnp.concatenate([a.reshape(-1) for a in arrays]), 0, [])
    subtotal = lax.psum(line, axis)
    for a in arrays:
        finished.append(subtotal[at : at + a.size].reshape(a.shape))
        at += a.size
    return tuple(finished)


def norm_stats(values):
    centre = jnp.mean(values, axis=-1, keepdims=True)
    centered = values - centre
    variance = jnp.mean(centered * centered, axis=-1, keepdims=True)
    inverse = lax.rsqrt(variance + epsilon)
    return (centered * inverse, inverse)


def norm_back(upstream, normal, inverse, weights):
    scaled = upstream * weights
    return inverse * (
        scaled
        - jnp.mean(scaled, axis=-1, keepdims=True)
        - normal * jnp.mean(scaled * normal, axis=-1, keepdims=True)
    )


def per_device(
    pair,
    cotangent,
    crop_length,
    in_gain,
    in_bias,
    proj_weight,
    gate_weight,
    out_gain,
    out_bias,
    out_weight,
):
    pair_tile = pair[0]
    upstream = cotangent[0]
    height, breadth, channels = pair_tile.shape
    hidden = out_weight.shape[0]
    row_first = lax.axis_index("row") * height
    col_first = lax.axis_index("col") * breadth
    crop_end = crop_length[0]
    row_live = (row_first + jnp.arange(height, dtype=jnp.int32) < crop_end).astype(jnp.float32)
    col_live = (col_first + jnp.arange(breadth, dtype=jnp.int32) < crop_end).astype(jnp.float32)
    live_mask = row_live[:, None, None] * col_live[None, :, None]
    in_hat, in_scale = norm_stats(pair_tile)
    normed = (in_hat * in_gain + in_bias).astype(jnp.bfloat16)
    flat_normed = normed.reshape(-1, channels)
    projected = jnp.dot(flat_normed, proj_weight, preferred_element_type=jnp.float32).reshape(
        height, breadth, 4 * hidden
    )
    left_sig = jax.nn.sigmoid(projected[..., :hidden])
    left_value = projected[..., hidden : 2 * hidden]
    right_sig = jax.nn.sigmoid(projected[..., 2 * hidden : 3 * hidden])
    right_value = projected[..., 3 * hidden :]
    left_factor = (left_sig * left_value * live_mask).astype(jnp.bfloat16)
    right_factor = (right_sig * right_value * live_mask).astype(jnp.bfloat16)
    right_rows = lax.all_gather(right_factor, "row", axis=0, tiled=True)
    right_turned = cut_exchange(right_rows, "col", 2, 0, 1)
    left_rows = lax.all_gather(left_factor, "col", axis=1, tiled=True)
    product = jnp.einsum(
        "ikh,jkh->ijh", left_rows, right_turned, preferred_element_type=jnp.float32
    )
    tri_hat, tri_scale = norm_stats(product)
    tri_normed = (tri_hat * out_gain + out_bias).astype(jnp.bfloat16)
    flat_tri = tri_normed.reshape(-1, hidden)
    out_value = jnp.dot(flat_tri, out_weight, preferred_element_type=jnp.float32)
    gate_value = jax.nn.sigmoid(
        jnp.dot(flat_normed, gate_weight, preferred_element_type=jnp.float32)
    )
    flat_up = upstream.reshape(-1, channels)
    d_out = (flat_up * gate_value).astype(jnp.bfloat16)
    d_gate = (flat_up * out_value * gate_value * (1.0 - gate_value)).astype(jnp.bfloat16)
    g_out_weight = jnp.dot(flat_tri.T, d_out, preferred_element_type=jnp.float32)
    d_tri_normed = jnp.dot(d_out, out_weight.T, preferred_element_type=jnp.float32).reshape(
        height, breadth, hidden
    )
    g_out_gain = jnp.sum(d_tri_normed * tri_hat, axis=(0, 1))
    g_out_bias = jnp.sum(d_tri_normed, axis=(0, 1))
    d_product = norm_back(d_tri_normed, tri_hat, tri_scale, out_gain).astype(jnp.bfloat16)
    grad_full = lax.all_gather(d_product, "col", axis=1, tiled=True)
    d_left = jnp.einsum("ijh,jkh->ikh", grad_full, right_rows, preferred_element_type=jnp.float32)
    d_right = lax.psum_scatter(
        jnp.einsum(
            "ijh,ikh->jkh", grad_full, left_factor, preferred_element_type=jnp.float32
        ).astype(jnp.bfloat16),
        "row",
        scatter_dimension=0,
        tiled=True,
    ).astype(jnp.float32)
    d_proj = (
        jnp.concatenate(
            [
                d_left * live_mask * left_value * left_sig * (1.0 - left_sig),
                d_left * live_mask * left_sig,
                d_right * live_mask * right_value * right_sig * (1.0 - right_sig),
                d_right * live_mask * right_sig,
            ],
            axis=-1,
        )
        .astype(jnp.bfloat16)
        .reshape(-1, 4 * hidden)
    )
    g_proj_weight = jnp.dot(flat_normed.T, d_proj, preferred_element_type=jnp.float32)
    g_gate_weight = jnp.dot(flat_normed.T, d_gate, preferred_element_type=jnp.float32)
    d_normed = (
        jnp.dot(d_proj, proj_weight.T, preferred_element_type=jnp.float32)
        + jnp.dot(d_gate, gate_weight.T, preferred_element_type=jnp.float32)
    ).reshape(height, breadth, channels)
    g_in_gain = jnp.sum(d_normed * in_hat, axis=(0, 1))
    g_in_bias = jnp.sum(d_normed, axis=(0, 1))
    grad_pair = norm_back(d_normed, in_hat, in_scale, in_gain)
    totals = packed_total(
        (g_in_gain, g_in_bias, g_proj_weight, g_gate_weight, g_out_gain, g_out_bias, g_out_weight),
        ("samp", "row", "col"),
    )
    factor = 1.0 / (breadth * lax.axis_size("col"))
    return (
        grad_pair[None],
        totals[0] * factor,
        totals[1] * factor,
        totals[2] * factor,
        totals[3] * factor,
        totals[4] * factor,
        totals[5] * factor,
        totals[6] * factor,
    )


def solution(mesh):
    return jax.shard_map(
        per_device,
        mesh=mesh,
        in_specs=(
            P("samp", "row", "col", None),
            P("samp", "row", "col", None),
            P("samp"),
            P(),
            P(),
            P(),
            P(),
            P(),
            P(),
            P(),
        ),
        out_specs=(P("samp", "row", "col", None), P(), P(), P(), P(), P(), P(), P()),
        check_vma=False,
    )
```

profile of v0, /device:TPU:1, one launch (start us, length us, event | category | flops | bytes accessed | tf_op | source)
XLA Modules:
  0.0 551.7 jit_solution(769624488051377025)
XLA Ops:
  12.4 2.5 multiply_convert_fusion.5
  16.4 42.1 %all-gather.4.cloned.1.call-done = bf16[320,40,128]{2,1,0:T(8,128)(2,1)} async-done(((bf16[80,40,128]{2,1,0:T(8,128)(2,1)}), bf16[320,40,128]{2,1,0:T(8,128)(2,1)}) %all-gather.4.cloned.1.call-update) | async-done | bytes 3276816 | tf_op jit(solution)/shard_map/all_gather | solution.py:95
  58.5 2.5 split.8
  61.0 6.1 %all-to-all-start = ((bf16[8,16,40,128]{3,2,1,0:T(8,128)(2,1)}), bf16[8,16,40,128]{3,2,1,0:T(8,128)(2,1)S(1)}, u32[]{:S(2)}, u32[]{:S(2)}) async-start(bf16[8,16,40,128]{3,2,1,0:T(8,128)(2,1)} %split.8), calls=%async_computation | async-start | bytes 2621440 | tf_op jit(solution)/shard_map/all_to_all | solution.py:31
  67.4 3.2 split.9
  70.6 23.4 %all-to-all-done = bf16[8,16,40,128]{3,2,1,0:T(8,128)(2,1)S(1)} async-done(((bf16[8,16,40,128]{3,2,1,0:T(8,128)(2,1)}), bf16[8,16,40,128]{3,2,1,0:T(8,128)(2,1)S(1)}, u32[]{:S(2)}, u32[]{:S(2)}) %all-to-all-start) | async-done | bytes 1310752 | tf_op jit(solution)/shard_map/all_to_all | solution.py:31
  94.0 4.3 all-to-all-start.1
  106.5 19.8 %all-to-all-done.1 = bf16[8,24,40,128]{3,2,1,0:T(8,128)(2,1)} async-done(((bf16[8,24,40,128]{3,2,1,0:T(8,128)(2,1)}), bf16[8,24,40,128]{3,2,1,0:T(8,128)(2,1)}, u32[]{:S(2)}, u32[]{:S(2)}) %all-to-all-start.1) | async-done | bytes 1966112 | tf_op jit(solution)/shard_map/all_to_all | solution.py:31
  129.1 4.4 copy.67
  133.5 38.1 %all-gather.6.cloned.1.call-done = bf16[80,320,128]{2,1,0:T(8,128)(2,1)} async-done(((bf16[80,40,128]{2,1,0:T(8,128)(2,1)}), bf16[80,320,128]{2,1,0:T(8,128)(2,1)}) %all-gather.6.cloned.1.call-update) | async-done | bytes 6553616 | tf_op jit(solution)/shard_map/all_gather | solution.py:97
  171.6 14.4 %copy.68 = bf16[80,320,128]{0,1,2:T(8,128)(2,1)} copy(bf16[80,320,128]{2,1,0:T(8,128)(2,1)} %all-gather.6.cloned.1.call-done) | data formatting | bytes 13107200 | tf_op jit(solution)/shard_map/all_gather | solution.py:97
  186.0 7.3 %bitcast_reduce_fusion = (f32[80,40]{0,1:T(8,128)S(1)}, f32[128,40,80]{2,1,0:T(8,128)S(1)}) fusion(bf16[40,320,128]{1,0,2:T(8,128)(2,1)} %copy.67, bf16[80,320,128]{0,1,2:T(8,128)(2,1)} %copy.68), kind=kOutput, calls=%fused_computation.27 | convolution fusion | flops 262550400 | bytes 11481600 | tf_op jit(solution)/shard_map/ikh,jkh->ijh/dot_general | solution.py:98
  194.1 3.6 multiply_reduce_fusion
  197.9 4.3 multiply_convert_fusion
  204.8 119.7 %all-gather.8.cloned.1.call-done = bf16[80,320,128]{0,1,2:T(8,128)(2,1)} async-done(((bf16[80,40,128]{0,1,2:T(8,128)(2,1)}), bf16[80,320,128]{0,1,2:T(8,128)(2,1)}) %all-gather.8.cloned.1.call-update) | async-done | bytes 6553616 | tf_op jit(solution)/shard_map/all_gather | solution.py:118
  324.5 9.2 %fusion.41 = bf16[128,40,320]{2,1,0:T(8,128)(2,1)} fusion(bf16[80,40,128]{0,1,2:T(8,128)(2,1)S(1)} %copy.79, bf16[80,320,128]{0,1,2:T(8,128)(2,1)} %all-gather.8.cloned.1.call-done), kind=kOutput, calls=%fused_computation.99 | convolution fusion | flops 262144000 | bytes 10649600 | tf_op jit(solution)/shard_map/ijh,ikh->jkh/dot_general | solution.py:121
  333.7 6.7 %copy.80 = bf16[128,40,320]{0,1,2:T(8,128)(2,1)} copy(bf16[128,40,320]{2,1,0:T(8,128)(2,1)} %fusion.41) | data formatting | bytes 6553600 | tf_op jit(solution)/shard_map/ijh,ikh->jkh/dot_general | solution.py:121
  342.3 4.9 copy.77
  347.2 2.8 copy.81
  355.7 5.4 fusion.40
  363.1 14.1 %reduce-scatter.2.cloned.1.call-done = bf16[80,40,128]{2,1,0:T(8,128)(2,1)} async-done(((bf16[320,40,128]{2,1,0:T(8,128)(2,1)}), bf16[80,40,128]{2,1,0:T(8,128)(2,1)}) %reduce-scatter.2.cloned.1.call-update) | async-done | bytes 819216 | tf_op jit(solution)/shard_map/reduce_scatter | solution.py:120
  377.2 4.4 multiply_convert_fusion.4
  397.5 4.1 subtract_multiply_fusion
  401.6 138.9 %all-reduce.2.cloned.1.call-done = f32[98816]{0:T(1024)} async-done(((f32[98816]{0:T(1024)}), f32[98816]{0:T(1024)}) %all-reduce.2.cloned.1.call-update) | async-done | bytes 395280 | tf_op jit(solution)/shard_map/psum | solution.py:37
  (127 shorter events, 50.2 us)
Async XLA Ops:
  7.2 3.9 copy-start
  7.2 51.4 %all-gather.4.cloned.1.call-start = ((), (), s32[]{:S(2)}) async-start(), calls=%async_computation.3 | async-start | bytes 4096000 | tf_op jit(solution)/shard_map/all_gather | solution.py:95
  7.2 3.8 copy-start.25
  7.3 3.8 copy-start.27
  12.4 3.3 copy-start.1
  15.7 155.9 %all-gather.6.cloned.1.call-start = ((), (), s32[]{:S(2)}) async-start(), calls=%async_computation.4 | async-start | bytes 7372800 | tf_op jit(solution)/shard_map/all_gather | solution.py:97
  61.0 32.9 %all-to-all-start = ((bf16[8,16,40,128]{3,2,1,0:T(8,128)(2,1)}), bf16[8,16,40,128]{3,2,1,0:T(8,128)(2,1)S(1)}, u32[]{:S(2)}, u32[]{:S(2)}) async-start(bf16[8,16,40,128]{3,2,1,0:T(8,128)(2,1)} %split.8), calls=%async_computation | async-start | bytes 2621440 | tf_op jit(solution)/shard_map/all_to_all | solution.py:31
  67.3 31.3 %copy-start.18 = (f32[3200]{0:T(1024)}, f32[3200]{0:T(1024)S(1)}, u32[]{:S(2)}) copy-start(f32[3200]{0:T(1024)S(1)} %rsqrt.22) | copy-start | bytes 38404
  67.4 31.2 %copy-start.20 = (f32[3200]{0:T(1024)}, f32[3200]{0:T(1024)S(1)}, u32[]{:S(2)}) copy-start(f32[3200]{0:T(1024)S(1)} %div.47) | copy-start | bytes 38404
  94.0 32.4 %all-to-all-start.1 = ((bf16[8,24,40,128]{3,2,1,0:T(8,128)(2,1)}), bf16[8,24,40,128]{3,2,1,0:T(8,128)(2,1)}, u32[]{:S(2)}, u32[]{:S(2)}) async-start(bf16[8,24,40,128]{3,2,1,0:T(8,128)(2,1)} %split.9), calls=%async_computation.1 | async-start | bytes 3932160 | tf_op jit(solution)/shard_map/all_to_all | solution.py:31
  98.3 226.1 %all-gather.8.cloned.1.call-start = ((), (), s32[]{:S(2)}) async-start(), calls=%async_computation.5 | async-start | bytes 11796480 | tf_op jit(solution)/shard_map/all_gather | solution.py:118
  194.1 3.8 copy-start.29
  202.2 175.0 %reduce-scatter.2.cloned.1.call-start = ((), (), s32[]{:S(2)}) async-start(), calls=%async_computation.6 | async-start | bytes 4096000 | tf_op jit(solution)/shard_map/reduce_scatter | solution.py:120
  340.4 200.2 %all-reduce.2.cloned.1.call-start = ((), (), s32[]{:S(2)}) async-start(), calls=%async_computation.7 | async-start | bytes 794624 | tf_op jit(solution)/shard_map/psum | solution.py:37
  347.2 2.9 copy-start.10
  347.2 3.9 copy-start.12
  351.1 3.0 copy-start.23
  363.1 18.5 %copy-start.3 = (f32[1,80,40,128]{3,2,1,0:T(8,128)S(1)}, f32[1,80,40,128]{3,2,1,0:T(8,128)}, u32[]{:S(2)}) copy-start(f32[1,80,40,128]{3,2,1,0:T(8,128)} %param.10) | copy-start | bytes 4915204
  363.1 18.5 %copy-start.26 = (f32[128]{0:T(128)S(1)}, f32[128]{0:T(128)}, u32[]{:S(2)}) copy-start(f32[128]{0:T(128)} %param.13) | copy-start | bytes 1540
  363.1 18.5 %copy-start.28 = (f32[128]{0:T(128)S(1)}, f32[128]{0:T(128)}, u32[]{:S(2)}) copy-start(f32[128]{0:T(128)} %param.14) | copy-start | bytes 1540
  383.4 6.3 %copy-start.15 = (f32[16384]{0:T(1024)S(1)}, f32[16384]{0:T(1024)}, u32[]{:S(2)}) copy-start(f32[16384]{0:T(1024)} %convolution_bitcast_fusion.1) | copy-start | bytes 196612
  383.4 7.8 %copy-start.31 = (f32[128]{0:T(128)S(1)}, f32[128]{0:T(128)}, u32[]{:S(2)}) copy-start(f32[128]{0:T(128)} %get-tuple-element.8) | copy-start | bytes 1540
  383.5 9.1 %copy-start.30 = (f32[128]{0:T(128)S(1)}, f32[128]{0:T(128)}, u32[]{:S(2)}) copy-start(f32[128]{0:T(128)} %get-tuple-element.13) | copy-start | bytes 1540
  383.5 10.4 %copy-start.14 = (f32[16384]{0:T(1024)S(1)}, f32[16384]{0:T(1024)}, u32[]{:S(2)}) copy-start(f32[16384]{0:T(1024)} %convolution_bitcast_fusion) | copy-start | bytes 196612
  (15 other events, 27.9 us)
Sparse Core Ops, SparseCore 0:
  15.8 42.7 all-gather.3
  61.0 110.5 all-gather.5
  202.4 122.0 all-gather.7
  340.5 36.6 reduce-scatter.1
  395.5 144.9 all-reduce.1
where the time goes:
time: 553 us; the launch traced here: 552 us
  waiting for transfers between devices  397 us (72%)
  local copies, waits for them, and re-layouts  62.9 us (11%)
  matrix products  35.3 us (6%)
  other arithmetic  30.6 us (6%)
  between operations  15 us (3%)
  starting transfers between devices  11.1 us (2%)
    psum x1, waiting for transfers between devices, packed_total(): subtotal = lax.psum(line, axis)  139 us
    all_gather x1, waiting for transfers between devices, per_device(): grad_full = lax.all_gather(d_product, 'col', axis=1, tiled=True)  120 us
    all_to_all x2, waiting for transfers between devices, cut_exchange(): lax.all_to_all(share, axis, split_axis=0, concat_axis=0, tiled=True)  43.2 us
    all_gather x1, waiting for transfers between devices, per_device(): right_rows = lax.all_gather(right_factor, 'row', axis=0, tiled=True)  42.1 us
    all_gather x1, waiting for transfers between devices, per_device(): left_rows = lax.all_gather(left_factor, 'col', axis=1, tiled=True)  38.1 us
    all_gather x1, local copies, waits for them, and re-layouts, per_device(): left_rows = lax.all_gather(left_factor, 'col', axis=1, tiled=True)  14.4 us
    reduce_scatter x1, waiting for transfers between devices, per_device(): lax.psum_scatter(jnp.einsum('ijh,ikh->jkh', grad_full, left_factor, prefe...  14.1 us
    unnamed x71, local copies, waits for them, and re-layouts  12.9 us
  transfers between devices with their start and end apart: 7, of which 7 were waited for; matrix products, arithmetic and copies ran while one was open for 9% of the time, Pallas kernels for 0%

commit v1 on v0

--- a/solution.py
+++ b/solution.py
@@ -2,6 +2,7 @@
 import jax.numpy as jnp
 from jax import lax
 from jax.sharding import PartitionSpec as P
+from jax.lax import all_to_all, psum
 
 epsilon = 1e-05
 
@@ -70,6 +71,13 @@
     out_bias,
     out_weight,
 ):
+
+    def series_divide(row_data):
+        local_part = psum(1, axis_name="col")
+        r2 = jnp.stack(local_part * [row_data])
+        shaped = all_to_all(r2, axis_name="col", split_axis=0, concat_axis=0)
+        return jnp.concatenate(shaped, axis=1)
+
     pair_tile = pair[0]
     upstream = cotangent[0]
     height, breadth, channels = pair_tile.shape
@@ -115,7 +123,7 @@
     g_out_gain = jnp.sum(d_tri_normed * tri_hat, axis=(0, 1))
     g_out_bias = jnp.sum(d_tri_normed, axis=(0, 1))
     d_product = norm_back(d_tri_normed, tri_hat, tri_scale, out_gain).astype(jnp.bfloat16)
-    grad_full = lax.all_gather(d_product, "col", axis=1, tiled=True)
+    grad_full = series_divide(d_product)
     d_left = jnp.einsum("ijh,jkh->ikh", grad_full, right_rows, preferred_element_type=jnp.float32)
     d_right = lax.psum_scatter(
         jnp.einsum(

time: 553 us -> 533 us (0.964)
  waiting for transfers between devices: 397 us -> 351 us
  local copies, waits for them, and re-layouts: 62.9 us -> 85.9 us
    all_gather x1 -> x0, waiting for transfers between devices: 120 us -> none  [per_device(): grad_full = lax.all_gather(d_product, 'col', axis=1, tiled=True)]
    all_to_all x0 -> x1, waiting for transfers between devices: none -> 72.3 us  [series_divide(): shaped = all_to_all(r2, axis_name='col', split_axis=0, concat_axis=0)]
    reshape x0 -> x1, local copies, waits for them, and re-layouts: none -> 10.7 us  [series_divide(): return jnp.concatenate(shaped, axis=1)]
    all_to_all x0 -> x1, local copies, waits for them, and re-layouts: none -> 7.48 us  [series_divide(): shaped = all_to_all(r2, axis_name='col', split_axis=0, concat_axis=0)]
where the time goes in v1:
time: 533 us; the launch traced here: 531 us
  waiting for transfers between devices  351 us (66%)
  local copies, waits for them, and re-layouts  85.9 us (16%)
  matrix products  32.4 us (6%)
  other arithmetic  30.6 us (6%)
  starting transfers between devices  15.9 us (3%)
  between operations  15 us (3%)
    psum x1, waiting for transfers between devices, packed_total(): subtotal = lax.psum(line, axis)  139 us
    all_to_all x1, waiting for transfers between devices, series_divide(): shaped = all_to_all(r2, axis_name='col', split_axis=0, concat_axis=0)  72.3 us
    all_to_all x2, waiting for transfers between devices, cut_exchange(): lax.all_to_all(share, axis, split_axis=0, concat_axis=0, tiled=True)  43.4 us
    all_gather x1, waiting for transfers between devices, per_device(): right_rows = lax.all_gather(right_factor, 'row', axis=0, tiled=True)  42.1 us
    all_gather x1, waiting for transfers between devices, per_device(): left_rows = lax.all_gather(left_factor, 'col', axis=1, tiled=True)  38 us
    reduce_scatter x1, waiting for transfers between devices, per_device(): lax.psum_scatter(jnp.einsum('ijh,ikh->jkh', grad_full, left_factor, prefe...  15.8 us
    all_gather x1, local copies, waits for them, and re-layouts, per_device(): left_rows = lax.all_gather(left_factor, 'col', axis=1, tiled=True)  14.4 us
    unnamed x71, local copies, waits for them, and re-layouts  12.1 us
  transfers between devices with their start and end apart: 7, of which 7 were waited for; matrix products, arithmetic and copies ran while one was open for 9% of the time, Pallas kernels for 0%

profile of v1, /device:TPU:1, one launch (start us, length us, event | category | flops | bytes accessed | tf_op | source)
XLA Modules:
  0.0 531.0 jit_solution(16127647783181152139)
XLA Ops:
  16.4 42.1 %all-gather.3.cloned.1.call-done = bf16[320,40,128]{2,1,0:T(8,128)(2,1)} async-done(((bf16[80,40,128]{2,1,0:T(8,128)(2,1)}), bf16[320,40,128]{2,1,0:T(8,128)(2,1)}) %all-gather.3.cloned.1.call-update) | async-done | bytes 3276816 | tf_op jit(solution)/shard_map/all_gather | solution.py:103
  61.0 6.1 %all-to-all-start = ((bf16[8,16,40,128]{3,2,1,0:T(8,128)(2,1)}), bf16[8,16,40,128]{3,2,1,0:T(8,128)(2,1)S(1)}, u32[]{:S(2)}, u32[]{:S(2)}) async-start(bf16[8,16,40,128]{3,2,1,0:T(8,128)(2,1)} %split.8), calls=%async_computation | async-start | bytes 2621440 | tf_op jit(solution)/shard_map/all_to_all | solution.py:32
  70.6 23.4 %all-to-all-done = bf16[8,16,40,128]{3,2,1,0:T(8,128)(2,1)S(1)} async-done(((bf16[8,16,40,128]{3,2,1,0:T(8,128)(2,1)}), bf16[8,16,40,128]{3,2,1,0:T(8,128)(2,1)S(1)}, u32[]{:S(2)}, u32[]{:S(2)}) %all-to-all-start) | async-done | bytes 1310752 | tf_op jit(solution)/shard_map/all_to_all | solution.py:32
  94.0 4.5 all-to-all-start.1
  106.4 20.0 %all-to-all-done.1 = bf16[8,24,40,128]{3,2,1,0:T(8,128)(2,1)} async-done(((bf16[8,24,40,128]{3,2,1,0:T(8,128)(2,1)}), bf16[8,24,40,128]{3,2,1,0:T(8,128)(2,1)}, u32[]{:S(2)}, u32[]{:S(2)}) %all-to-all-start.1) | async-done | bytes 1966112 | tf_op jit(solution)/shard_map/all_to_all | solution.py:32
  129.2 4.3 copy.75
  133.5 38.0 %all-gather.5.cloned.1.call-done = bf16[80,320,128]{2,1,0:T(8,128)(2,1)} async-done(((bf16[80,40,128]{2,1,0:T(8,128)(2,1)}), bf16[80,320,128]{2,1,0:T(8,128)(2,1)}) %all-gather.5.cloned.1.call-update) | async-done | bytes 6553616 | tf_op jit(solution)/shard_map/all_gather | solution.py:105
  171.6 14.4 %copy.76 = bf16[80,320,128]{0,1,2:T(8,128)(2,1)} copy(bf16[80,320,128]{2,1,0:T(8,128)(2,1)} %all-gather.5.cloned.1.call-done) | data formatting | bytes 13107200 | tf_op jit(solution)/shard_map/all_gather | solution.py:105
  186.0 7.3 %bitcast_reduce_fusion = (f32[80,40]{0,1:T(8,128)S(1)}, f32[128,40,80]{2,1,0:T(8,128)S(1)}) fusion(bf16[40,320,128]{1,0,2:T(8,128)(2,1)} %copy.75, bf16[80,320,128]{0,1,2:T(8,128)(2,1)} %copy.76), kind=kOutput, calls=%fused_computation.27 | convolution fusion | flops 262550400 | bytes 11481600 | tf_op jit(solution)/shard_map/ikh,jkh->ijh/dot_general | solution.py:106
  194.1 3.6 multiply_reduce_fusion
  197.8 4.4 multiply_convert_fusion
  204.7 3.6 stack.2
  208.3 4.9 all-to-all-start.2
  214.9 72.3 %all-to-all-done.2 = bf16[8,80,40,128]{3,2,1,0:T(8,128)(2,1)} async-done(((bf16[8,80,40,128]{3,2,1,0:T(8,128)(2,1)}), bf16[8,80,40,128]{3,2,1,0:T(8,128)(2,1)}, u32[]{:S(2)}, u32[]{:S(2)}) %all-to-all-start.2) | async-done | bytes 6553632 | tf_op jit(solution)/shard_map/all_to_all | solution.py:78
  287.1 7.5 %copy.86 = bf16[8,80,40,128]{3,2,0,1:T(8,128)(2,1)} copy(bf16[8,80,40,128]{3,2,1,0:T(8,128)(2,1)} %all-to-all-done.2) | data formatting | bytes 13107200 | tf_op jit(solution)/shard_map/all_to_all | solution.py:78
  294.6 10.7 %copy.88 = bf16[80,320,128]{1,0,2:T(8,128)(2,1)} copy(bf16[80,320,128]{2,1,0:T(8,128)(2,1)} %bitcast.97) | data formatting | bytes 13107200 | tf_op jit(solution)/shard_map/reshape | solution.py:79
  305.3 6.6 %fusion.41 = bf16[128,40,320]{2,1,0:T(8,128)(2,1)} fusion(bf16[80,40,128]{0,1,2:T(8,128)(2,1)S(1)} %copy.90, bf16[80,320,128]{1,0,2:T(8,128)(2,1)} %copy.88), kind=kOutput, calls=%fused_computation.99 | convolution fusion | flops 262144000 | bytes 10649600 | tf_op jit(solution)/shard_map/ijh,ikh->jkh/dot_general | solution.py:129
  311.9 6.6 %copy.92 = bf16[128,40,320]{0,1,2:T(8,128)(2,1)} copy(bf16[128,40,320]{2,1,0:T(8,128)(2,1)} %fusion.41) | data formatting | bytes 6553600 | tf_op jit(solution)/shard_map/ijh,ikh->jkh/dot_general | solution.py:129
  320.5 4.9 copy.87
  333.6 5.1 fusion.40
  340.8 15.8 %reduce-scatter.2.cloned.1.call-done = bf16[80,40,128]{2,1,0:T(8,128)(2,1)} async-done(((bf16[320,40,128]{2,1,0:T(8,128)(2,1)}), bf16[80,40,128]{2,1,0:T(8,128)(2,1)}) %reduce-scatter.2.cloned.1.call-update) | async-done | bytes 819216 | tf_op jit(solution)/shard_map/reduce_scatter | solution.py:128
  356.6 4.4 multiply_convert_fusion.4
  376.9 4.1 subtract_multiply_fusion
  381.0 138.9 %all-reduce.2.cloned.1.call-done = f32[98816]{0:T(1024)} async-done(((f32[98816]{0:T(1024)}), f32[98816]{0:T(1024)}) %all-reduce.2.cloned.1.call-update) | async-done | bytes 395280 | tf_op jit(solution)/shard_map/psum | solution.py:38
  (130 shorter events, 62.4 us)
Async XLA Ops:
  7.2 3.9 copy-start
  7.2 51.3 %all-gather.3.cloned.1.call-start = ((), (), s32[]{:S(2)}) async-start(), calls=%async_computation.4 | async-start | bytes 4096000 | tf_op jit(solution)/shard_map/all_gather | solution.py:103
  7.2 3.8 copy-start.25
  7.3 3.8 copy-start.27
  12.4 3.3 copy-start.1
  15.7 155.9 %all-gather.5.cloned.1.call-start = ((), (), s32[]{:S(2)}) async-start(), calls=%async_computation.5 | async-start | bytes 7372800 | tf_op jit(solution)/shard_map/all_gather | solution.py:105
  61.0 32.9 %all-to-all-start = ((bf16[8,16,40,128]{3,2,1,0:T(8,128)(2,1)}), bf16[8,16,40,128]{3,2,1,0:T(8,128)(2,1)S(1)}, u32[]{:S(2)}, u32[]{:S(2)}) async-start(bf16[8,16,40,128]{3,2,1,0:T(8,128)(2,1)} %split.8), calls=%async_computation | async-start | bytes 2621440 | tf_op jit(solution)/shard_map/all_to_all | solution.py:32
  67.3 31.2 %copy-start.18 = (f32[3200]{0:T(1024)}, f32[3200]{0:T(1024)S(1)}, u32[]{:S(2)}) copy-start(f32[3200]{0:T(1024)S(1)} %rsqrt.22) | copy-start | bytes 38404
  67.4 31.1 %copy-start.20 = (f32[3200]{0:T(1024)}, f32[3200]{0:T(1024)S(1)}, u32[]{:S(2)}) copy-start(f32[3200]{0:T(1024)S(1)} %div.47) | copy-start | bytes 38404
  94.0 32.5 %all-to-all-start.1 = ((bf16[8,24,40,128]{3,2,1,0:T(8,128)(2,1)}), bf16[8,24,40,128]{3,2,1,0:T(8,128)(2,1)}, u32[]{:S(2)}, u32[]{:S(2)}) async-start(bf16[8,24,40,128]{3,2,1,0:T(8,128)(2,1)} %split.9), calls=%async_computation.1 | async-start | bytes 3932160 | tf_op jit(solution)/shard_map/all_to_all | solution.py:32
  194.1 3.8 copy-start.29
  208.3 5.2 copy-start.6
  208.3 78.8 %all-to-all-start.2 = ((bf16[8,80,40,128]{3,2,1,0:T(8,128)(2,1)}), bf16[8,80,40,128]{3,2,1,0:T(8,128)(2,1)}, u32[]{:S(2)}, u32[]{:S(2)}) async-start(bf16[8,80,40,128]{3,2,1,0:T(8,128)(2,1)} %stack.2), calls=%async_computation.2 | async-start | bytes 13107200 | tf_op jit(solution)/shard_map/all_to_all | solution.py:78
  213.2 143.4 %reduce-scatter.2.cloned.1.call-start = ((), (), s32[]{:S(2)}) async-start(), calls=%async_computation.6 | async-start | bytes 4096000 | tf_op jit(solution)/shard_map/reduce_scatter | solution.py:128
  318.6 201.3 %all-reduce.2.cloned.1.call-start = ((), (), s32[]{:S(2)}) async-start(), calls=%async_computation.7 | async-start | bytes 794624 | tf_op jit(solution)/shard_map/psum | solution.py:38
  325.4 3.7 copy-start.12
  329.1 3.0 copy-start.23
  340.8 20.2 %copy-start.3 = (f32[1,80,40,128]{3,2,1,0:T(8,128)S(1)}, f32[1,80,40,128]{3,2,1,0:T(8,128)}, u32[]{:S(2)}) copy-start(f32[1,80,40,128]{3,2,1,0:T(8,128)} %param.10) | copy-start | bytes 4915204
  340.8 20.2 %copy-start.26 = (f32[128]{0:T(128)S(1)}, f32[128]{0:T(128)}, u32[]{:S(2)}) copy-start(f32[128]{0:T(128)} %param.13) | copy-start | bytes 1540
  340.8 20.2 %copy-start.28 = (f32[128]{0:T(128)S(1)}, f32[128]{0:T(128)}, u32[]{:S(2)}) copy-start(f32[128]{0:T(128)} %param.14) | copy-start | bytes 1540
  362.8 6.3 %copy-start.15 = (f32[16384]{0:T(1024)S(1)}, f32[16384]{0:T(1024)}, u32[]{:S(2)}) copy-start(f32[16384]{0:T(1024)} %convolution_bitcast_fusion.1) | copy-start | bytes 196612
  362.8 7.8 %copy-start.31 = (f32[128]{0:T(128)S(1)}, f32[128]{0:T(128)}, u32[]{:S(2)}) copy-start(f32[128]{0:T(128)} %get-tuple-element.8) | copy-start | bytes 1540
  362.8 9.1 %copy-start.30 = (f32[128]{0:T(128)S(1)}, f32[128]{0:T(128)}, u32[]{:S(2)}) copy-start(f32[128]{0:T(128)} %get-tuple-element.13) | copy-start | bytes 1540
  362.8 10.4 %copy-start.14 = (f32[16384]{0:T(1024)S(1)}, f32[16384]{0:T(1024)}, u32[]{:S(2)}) copy-start(f32[16384]{0:T(1024)} %convolution_bitcast_fusion) | copy-start | bytes 196612
  (15 other events, 29.2 us)
Sparse Core Ops, SparseCore 0:
  15.8 42.7 all-gather.2
  60.9 110.5 all-gather.4
  318.7 37.8 reduce-scatter.1
  374.9 144.9 all-reduce.1
